TPU v7x, 32 devices: a whole 2x2x4 slice. The times are simulated.
32 devices in a mesh: shard: 8 (over z, core), rep: 4 (over y, x).
Axes of the slice: x: 2, y: 2, z: 4, core: 2. Of those that a mesh axis runs over, the one named last changes fastest.
Arguments:
- tokens: bfloat16 [12288, 5120], P(('shard', 'rep')), may hold values from -700 to 700
- norm_gain: float32 [5120], replicated, may hold values from 0.1 to 1.9
- key_bias: float32 [1024], replicated, may hold values from -4 to 4
- key_weight: bfloat16 [8192, 1024], P('shard'), may hold values from -0.078125 to 0.078125
- cotangent: bfloat16 [12288, 1024], P(('shard', 'rep')), may hold values from -40 to 40
- block_slot: int32 [40], replicated, may hold values from 0 to 63, as said below
Outputs:
- projected: bfloat16 [12288, 1024], P(('shard', 'rep'))
- token_grad: bfloat16 [12288, 5120], P(('shard', 'rep'))
- weight_grad: float32 [8192, 1024], P('shard')
- gain_grad: float32 [5120], replicated
- bias_grad: float32 [1024], replicated
Inputs may be any that keep to these rules, and one draw needn't show every extreme that they name: Entries are distinct; block b lies on the device of shard with index block_slot[b] // 8, at its local slot block_slot[b] % 8; in every draw some device holds 8 blocks.
All inputs are finite; a program needn't handle non-finite values.
Results may differ from a plain program's by a relative error of at most 0.013.
Values may be sent and summed in bfloat16 or wider, within the bound.
A program may use at most 128 MiB of HBM per device.

v0:
```python
import jax
import jax.numpy as jnp
from jax import lax
from jax.sharding import PartitionSpec as P

BLK = 128
EPS = 1e-06


def normalize(tokens, norm_gain):
    values = tokens.astype(jnp.float32)
    inv_rms = lax.rsqrt(jnp.mean(values * values, axis=-1, keepdims=True) + EPS)
    normed = (values * inv_rms * norm_gain).astype(jnp.bfloat16)
    return (values, inv_rms, normed)


def token_backward(values, inv_rms, grad_normed, norm_gain):
    scaled = grad_normed * norm_gain
    inner = jnp.mean(scaled * values, axis=-1, keepdims=True)
    return (inv_rms * (scaled - values * inv_rms * inv_rms * inner)).astype(jnp.bfloat16)


def local(tokens, norm_gain, key_bias, key_weight, cotangent, block_slot):
    values, inv_rms, normed = normalize(tokens, norm_gain)
    row_count = tokens.shape[0]
    width = tokens.shape[1]
    local_rows = key_weight.shape[0]
    shard_count = lax.axis_size("shard")
    replicas = lax.axis_size("rep")
    slot_total = shard_count * local_rows // BLK
    block_count = width // BLK
    block_of_slot = (
        jnp.full((slot_total,), -1, jnp.int32)
        .at[block_slot]
        .set(jnp.arange(block_count, dtype=jnp.int32))
    )
    present = block_of_slot >= 0
    normed_blocks = normed.reshape(row_count, block_count, BLK)
    normed_slots = jnp.take(normed_blocks, jnp.maximum(block_of_slot, 0), axis=1)
    normed_slots = jnp.where(present[None, :, None], normed_slots, jnp.zeros((), jnp.bfloat16))
    normed_slots = normed_slots.reshape(row_count, slot_total * BLK)
    piece = lax.all_gather(key_weight, "shard", axis=0, tiled=True)
    columns = normed_slots
    forward_sum = jnp.dot(columns, piece, preferred_element_type=jnp.float32)
    backward_part = lax.dot_general(
        cotangent, piece, (((1,), (1,)), ((), ())), preferred_element_type=jnp.float32
    )
    projected = (forward_sum + key_bias).astype(jnp.bfloat16)
    grad_normed = jnp.take(backward_part.reshape(row_count, slot_total, BLK), block_slot, axis=1)
    grad_normed = grad_normed.reshape(row_count, width)
    token_grad = token_backward(values, inv_rms, grad_normed, norm_gain)
    grad_scale = float(row_count * shard_count * replicas) ** (-0.5)
    columns = normed_slots
    group_sum = lax.psum_scatter(
        (
            lax.dot_general(
                columns, cotangent, (((0,), (0,)), ((), ())), preferred_element_type=jnp.float32
            )
            * grad_scale
        ).astype(jnp.bfloat16),
        "shard",
        scatter_dimension=0,
        tiled=True,
    ).astype(jnp.float32)
    gain_part = jnp.sum(grad_normed * values * inv_rms, axis=0) * grad_scale
    bias_part = jnp.sum(cotangent.astype(jnp.float32), axis=0) * grad_scale
    weight_grad = lax.psum(group_sum, "rep")
    gain_grad, bias_grad = lax.psum((gain_part, bias_part), ("shard", "rep"))
    return (projected, token_grad, weight_grad, gain_grad, bias_grad)


def solution(mesh):
    return jax.shard_map(
        local,
        mesh=mesh,
        in_specs=(
            P(("shard", "rep"), None),
            P(),
            P(),
            P("shard", None),
            P(("shard", "rep"), None),
            P(),
        ),
        out_specs=(
            P(("shard", "rep"), None),
            P(("shard", "rep"), None),
            P("shard", None),
            P(),
            P(),
        ),
        check_vma=False,
    )
```

profile of v0, /device:TPU:16, one launch (start us, length us, event | category | flops | bytes accessed | tf_op | source)
XLA Modules:
  0.0 578.5 jit_solution(7815864115164983269)
XLA Ops:
  7.2 0.0 copy-start.6
  7.2 0.0 copy-start.3
  7.2 0.0 all-gather.2.cloned.1.call-start
  7.2 0.7 all-gather.2.cloned.1.call-update
  7.9 0.0 reduce-scatter.2.cloned.1.call-start
  8.0 6.3 %copy.12 = bf16[384,5120]{0,1:T(8,128)(2,1)} copy(bf16[384,5120]{1,0:T(8,128)(2,1)} %param.6) | data formatting | bytes 7864320 | tf_op args[0]
  14.2 0.0 copy-done.6
  14.2 0.7 scatter_custom_fusion
  15.0 3.0 fusion.7
  18.1 0.1 broadcast_bitcast_fusion.2
  18.1 0.1 broadcast_bitcast_fusion
  18.2 141.7 %all-gather.2.cloned.1.call-done = bf16[8192,1024]{1,0:T(8,128)(2,1)} async-done(((bf16[1024,1024]{1,0:T(8,128)(2,1)}), bf16[8192,1024]{1,0:T(8,128)(2,1)}) %all-gather.2.cloned.1.call-update) | async-done | bytes 16777232 | tf_op jit(solution)/shard_map/all_gather | solution.py:42
  160.0 12.9 %convolution_bitcast_fusion = f32[48,64,8,128]{3,2,1,0:T(8,128)} fusion(bf16[384,1024]{1,0:T(8,128)(2,1)S(1)} %copy-done.3, bf16[8192,1024]{1,0:T(8,128)(2,1)} %all-gather.2.cloned.1.call-done), kind=kOutput, calls=%fused_computation.24 | convolution fusion | flops 6442450944 | bytes 30146560 | tf_op jit(solution)/shard_map/dot_general | solution.py:45
  172.9 10.8 %copy.20 = f32[48,64,8,128]{3,2,0,1:T(8,128)} copy(f32[48,64,8,128]{3,2,1,0:T(8,128)} %convolution_bitcast_fusion) | data formatting | bytes 25165824 | tf_op jit(solution)/shard_map/reshape | solution.py:49
  183.7 8.7 %gather_fusion.1 = f32[40,384,128]{2,1,0:T(8,128)} fusion(f32[384,64,128]{2,0,1:T(8,128)} %bitcast.34, s32[1024]{0:T(1024)S(1)} %pad_clamp_fusion), kind=kCustom, calls=%fused_computation.1 | custom fusion | bytes 15728800 | tf_op jit(solution)/shard_map/jit(_take)/gather | solution.py:49
  192.4 9.1 %copy.16 = f32[384,40,128]{0,2,1:T(8,128)} copy(f32[384,40,128]{2,0,1:T(8,128)} %bitcast.35) | data formatting | bytes 15728640 | tf_op jit(solution)/shard_map/jit(_take)/gather | solution.py:49
  201.5 8.8 %fusion.10 = (f32[5120]{0:T(1024)S(1)}, f32[384]{0:T(512)S(1)}) fusion(bf16[384,5120]{0,1:T(8,128)(2,1)} %copy.12, f32[384,40,128]{0,2,1:T(8,128)} %copy.16, f32[384]{0:T(512)S(1)} %add_rsqrt_fusion, pred[5120]{0:T(1024)(128)(4,1)S(1)} %broadcast_bitcast_fusion.2, f32[5120]{0:T(1024)S(1)} %copy-done.4), kind=kLoop, calls=%fused_computation.19 | loop fusion | flops 15723136 | bytes 11845632 | tf_op jit(solution)/shard_map/reduce_sum | solution.py:65
  210.3 5.5 fusion.6
  215.8 6.3 %copy.13 = bf16[384,40,128]{2,0,1:T(8,128)(2,1)} copy(bf16[384,40,128]{0,2,1:T(8,128)(2,1)} %bitcast.37) | data formatting | bytes 7864320 | tf_op jit(solution)/shard_map/reshape | solution.py:38
  222.1 6.1 %gather_fusion = bf16[64,384,128]{2,1,0:T(8,128)(2,1)} fusion(bf16[384,40,128]{2,0,1:T(8,128)(2,1)} %copy.13, s32[1024]{0:T(1024)S(1)} %pad_clamp_fusion.1), kind=kCustom, calls=%fused_computation | custom fusion | bytes 12583168 | tf_op jit(solution)/shard_map/jit(_take)/gather | solution.py:39
  228.2 8.6 %copy.14 = bf16[384,64,128]{0,2,1:T(8,128)(2,1)} copy(bf16[384,64,128]{2,0,1:T(8,128)(2,1)} %bitcast.36) | data formatting | bytes 12582912 | tf_op jit(solution)/shard_map/jit(_take)/gather | solution.py:39
  236.8 6.9 %fusion.12 = bf16[384,8192]{0,1:T(8,128)(2,1)S(1)} fusion(bf16[384,64,128]{0,2,1:T(8,128)(2,1)} %copy.14, pred[8192]{0:T(1024)(128)(4,1)S(1)} %get-tuple-element.18, pred[8192]{0:T(1024)(128)(4,1)S(1)} %get-tuple-element.19), kind=kLoop, calls=%fused_computation.23 | loop fusion | flops 6291456 | bytes 12599296 | tf_op jit(solution)/shard_map/jit(_where)/select_n | solution.py:40
  243.7 2.6 copy-done.2
  246.3 11.7 %multiply_convert_fusion = bf16[8192,1024]{1,0:T(8,128)(2,1)} fusion(bf16[384,8192]{0,1:T(8,128)(2,1)S(1)} %fusion.12, bf16[384,1024]{1,0:T(8,128)(2,1)S(1)} %copy-done.3), kind=kOutput, calls=%fused_computation.3 | convolution fusion | flops 6459228160 | bytes 23855104 | tf_op jit(solution)/shard_map/dot_general | solution.py:56
  258.0 0.0 reduce-scatter.2.cloned.1.call-update
  258.0 0.0 copy-start.5
  258.0 0.1 convert_reduce_fusion
  258.2 6.3 %copy.17 = bf16[384,5120]{1,0:T(8,128)(2,1)} copy(bf16[384,5120]{0,1:T(8,128)(2,1)} %get-tuple-element.14) | data formatting | bytes 7864320
  264.4 42.3 %all-reduce = (f32[5120]{0:T(1024)}, f32[1024]{0:T(1024)}) all-reduce(f32[5120]{0:T(1024)S(1)} %broadcast_multiply_fusion, f32[1024]{0:T(1024)S(1)} %broadcast_multiply_fusion.1), channel_id=1, replica_groups=mesh['shard'=8,'rep'=4] {'shard','rep'}, use_global_device_ids=true, to_apply=%region_6.7 | all-reduce | flops 6144 | bytes 49152 | tf_op jit(solution)/shard_map/psum | solution.py:68
  306.7 13.0 %add_convert_fusion = bf16[384,1024]{1,0:T(8,128)(2,1)} fusion(bf16[384,8192]{0,1:T(8,128)(2,1)} %copy-done.2, bf16[8192,1024]{1,0:T(8,128)(2,1)} %all-gather.2.cloned.1.call-done, f32[1024]{0:T(1024)S(1)} %copy-done.5), kind=kOutput, calls=%fused_computation.26 | convolution fusion | flops 6443237376 | bytes 23859200 | tf_op jit(solution)/shard_map/dot_general | solution.py:44
  319.7 105.2 %reduce-scatter.2.cloned.1.call-done = bf16[1024,1024]{1,0:T(8,128)(2,1)} async-done(((bf16[8192,1024]{1,0:T(8,128)(2,1)}), bf16[1024,1024]{1,0:T(8,128)(2,1)}) %reduce-scatter.2.cloned.1.call-update) | async-done | bytes 2097168 | tf_op jit(solution)/shard_map/reduce_scatter | solution.py:54
  424.9 146.8 %all-reduce.2 = f32[1024,1024]{1,0:T(8,128)} all-reduce(bf16[1024,1024]{1,0:T(8,128)(2,1)} %reduce-scatter.2.cloned.1.call-done), channel_id=1, replica_groups=mesh['shard'=8,'rep'=4] {'rep'}, use_global_device_ids=true, to_apply=%region_4.5 | all-reduce | flops 1048576 | bytes 6291456 | tf_op jit(solution)/shard_map/psum | solution.py:67
  (20 shorter events, 0.1 us)
Async XLA Ops:
  7.2 7.1 %copy-start.6 = (s32[40]{0:T(128)S(1)}, s32[40]{0:T(128)}, u32[]{:S(2)}) copy-start(s32[40]{0:T(128)} %param.11) | copy-start | bytes 484
  7.2 152.8 %copy-start.3 = (bf16[384,1024]{1,0:T(8,128)(2,1)S(1)}, bf16[384,1024]{1,0:T(8,128)(2,1)}, u32[]{:S(2)}) copy-start(bf16[384,1024]{1,0:T(8,128)(2,1)} %param.10) | copy-start | bytes 2359300
  7.2 152.8 %all-gather.2.cloned.1.call-start = ((), (), s32[]{:S(2)}) async-start(), calls=%async_computation.1 | async-start | bytes 18874368 | tf_op jit(solution)/shard_map/all_gather | solution.py:42
  7.9 417.0 %reduce-scatter.2.cloned.1.call-start = ((), (), s32[]{:S(2)}) async-start(), calls=%async_computation.2 | async-start | bytes 18874368 | tf_op jit(solution)/shard_map/reduce_scatter | solution.py:54
  192.4 9.1 %copy-start.4 = (f32[5120]{0:T(1024)S(1)}, f32[5120]{0:T(1024)}, u32[]{:S(2)}) copy-start(f32[5120]{0:T(1024)} %param.7) | copy-start | bytes 61444
  201.5 8.8 %copy-start = (f32[384,40,128]{0,2,1:T(8,128)S(1)}, f32[384,40,128]{0,2,1:T(8,128)}, u32[]{:S(2)}) copy-start(f32[384,40,128]{0,2,1:T(8,128)} %copy.16) | copy-start | bytes 23592964
  201.5 8.8 %copy-start.1 = (bf16[384,5120]{0,1:T(8,128)(2,1)S(1)}, bf16[384,5120]{0,1:T(8,128)(2,1)}, u32[]{:S(2)}) copy-start(bf16[384,5120]{0,1:T(8,128)(2,1)} %copy.12) | copy-start | bytes 11796484
  243.7 2.6 copy-start.2
  258.0 48.7 %copy-start.5 = (f32[1024]{0:T(1024)S(1)}, f32[1024]{0:T(1024)}, u32[]{:S(2)}) copy-start(f32[1024]{0:T(1024)} %param.8) | copy-start | bytes 12292
Sparse Core Ops, SparseCore 0:
  9.6 150.3 all-gather.1
  258.1 166.7 reduce-scatter.1
where the time goes:
time: 580 us; the launch traced here: 579 us
  waiting for transfers between devices  248 us (43%)
  blocking collectives  189 us (33%)
  local copies, waits for them, and re-layouts  65.7 us (11%)
  matrix products  37.5 us (6%)
  other arithmetic  24.4 us (4%)
  between operations  14.2 us (2%)
    psum x1, blocking collectives, local(): weight_grad = lax.psum(group_sum, 'rep')  147 us
    all_gather x1, waiting for transfers between devices, local(): piece = lax.all_gather(key_weight, 'shard', axis=0, tiled=True)  142 us
    reduce_scatter x1, waiting for transfers between devices, local(): lax.psum_scatter((lax.dot_general(columns, cotangent, (((0,), (0,)), ((),...  105 us
    psum x1, blocking collectives, local(): gain_grad, bias_grad = lax.psum((gain_part, bias_part), ('shard', 'rep'))  42.3 us
    gather x2, local copies, waits for them, and re-layouts, local(): jnp.take(backward_part.reshape(row_count, slot_total, BLK), block_slot, a...  17.8 us
    unnamed x16, local copies, waits for them, and re-layouts  15.2 us
    gather x2, local copies, waits for them, and re-layouts, local(): jnp.take(normed_blocks, jnp.maximum(block_of_slot, 0), axis=1)  14.7 us
    dot_general x1, matrix products, local(): forward_sum = jnp.dot(columns, piece, preferred_element_type=jnp.float32)  13 us
  transfers between devices with their start and end apart: 2, of which 2 were waited for; matrix products, arithmetic and copies ran while one was open for 5% of the time, Pallas kernels for 0%

commit v1 on v0

--- a/solution.py
+++ b/solution.py
@@ -39,7 +39,13 @@
     normed_slots = jnp.take(normed_blocks, jnp.maximum(block_of_slot, 0), axis=1)
     normed_slots = jnp.where(present[None, :, None], normed_slots, jnp.zeros((), jnp.bfloat16))
     normed_slots = normed_slots.reshape(row_count, slot_total * BLK)
-    piece = lax.all_gather(key_weight, "shard", axis=0, tiled=True)
+    peers = lax.axis_size("shard")
+    held, blocks = (key_weight, [key_weight])
+    for _ in range(peers - 1):
+        held = lax.ppermute(held, "shard", [(i, (i + 1) % peers) for i in range(peers)])
+        blocks.insert(0, held)
+    row_of_blocks = jnp.concatenate(blocks, axis=0)
+    piece = jnp.roll(row_of_blocks, (lax.axis_index("shard") + 1) * key_weight.shape[0], axis=0)
     columns = normed_slots
     forward_sum = jnp.dot(columns, piece, preferred_element_type=jnp.float32)
     backward_part = lax.dot_general(

time: 580 us -> 633 us (1.091)
  waiting for transfers between devices: 248 us -> 273 us
  local copies, waits for them, and re-layouts: 65.7 us -> 81.7 us
  blocking collectives: 189 us -> 200 us
    ppermute x0 -> x7, waiting for transfers between devices: none -> 168 us  [local(): lax.ppermute(held, 'shard', [(i, (i + 1) % peers) for i in range(peers)])]
    all_gather x1 -> x0, waiting for transfers between devices: 142 us -> none  [local(): piece = lax.all_gather(key_weight, 'shard', axis=0, tiled=True)]
    unnamed x16 -> x49, local copies, waits for them, and re-layouts: 15.2 us -> 49.7 us
    reshape x1 -> x0, local copies, waits for them, and re-layouts: 10.8 us -> none  [local(): backward_part.reshape(row_count, slot_total, BLK)]
    psum x1, blocking collectives: 42.3 us -> 52.8 us  [local(): gain_grad, bias_grad = lax.psum((gain_part, bias_part), ('shard', 'rep'))]
    gather x2 -> x1, local copies, waits for them, and re-layouts: 17.8 us -> 8.71 us  [local(): jnp.take(backward_part.reshape(row_count, slot_total, BLK), block_slot, a...]
  transfers between devices with their start and end apart: 2 -> 8, of which waited for: 2 -> 8; matrix products, arithmetic and copies ran while one was open for 5% -> 5% of each run, Pallas kernels for 0% -> 0%
where the time goes in v1:
time: 633 us; the launch traced here: 632 us
  waiting for transfers between devices  273 us (43%)
  blocking collectives  200 us (32%)
  local copies, waits for them, and re-layouts  81.7 us (13%)
  matrix products  39.7 us (6%)
  other arithmetic  23.6 us (4%)
  between operations  14.2 us (2%)
    ppermute x7, waiting for transfers between devices, local(): lax.ppermute(held, 'shard', [(i, (i + 1) % peers) for i in range(peers)])  168 us
    psum x1, blocking collectives, local(): weight_grad = lax.psum(group_sum, 'rep')  147 us
    reduce_scatter x1, waiting for transfers between devices, local(): lax.psum_scatter((lax.dot_general(columns, cotangent, (((0,), (0,)), ((),...  105 us
    psum x1, blocking collectives, local(): gain_grad, bias_grad = lax.psum((gain_part, bias_part), ('shard', 'rep'))  52.8 us
    unnamed x49, local copies, waits for them, and re-layouts  49.7 us
    dot_general x1, matrix products, local(): lax.dot_general(cotangent, piece, (((1,), (1,)), ((), ())), preferred_ele...  15.1 us
    gather x2, local copies, waits for them, and re-layouts, local(): jnp.take(normed_blocks, jnp.maximum(block_of_slot, 0), axis=1)  14.7 us
    dot_general x1, matrix products, local(): forward_sum = jnp.dot(columns, piece, preferred_element_type=jnp.float32)  13 us
  transfers between devices with their start and end apart: 8, of which 8 were waited for; matrix products, arithmetic and copies ran while one was open for 5% of the time, Pallas kernels for 0%

profile of v1, /device:TPU:16, one launch (start us, length us, event | category | flops | bytes accessed | tf_op | source)
XLA Modules:
  0.0 632.4 jit_solution(74251185136835088)
XLA Ops:
  7.3 25.7 %collective-permute-done = bf16[1024,1024]{1,0:T(8,128)(2,1)S(1)} collective-permute-done((bf16[1024,1024]{1,0:T(8,128)(2,1)}, bf16[1024,1024]{1,0:T(8,128)(2,1)S(1)}, u32[]{:S(2)}, u32[]{:S(2)}) %collective-permute-start) | collective-permute-done | bytes 2097184 | tf_op jit(solution)/shard_map/ppermute | solution.py:45
  32.9 25.5 %collective-permute-done.1 = bf16[1024,1024]{1,0:T(8,128)(2,1)S(1)} collective-permute-done((bf16[1024,1024]{1,0:T(8,128)(2,1)S(1)}, bf16[1024,1024]{1,0:T(8,128)(2,1)S(1)}, u32[]{:S(2)}, u32[]{:S(2)}) %collective-permute-start.1) | collective-permute-done | bytes 2097184 | tf_op jit(solution)/shard_map/ppermute | solution.py:45
  59.7 25.5 %collective-permute-done.2 = bf16[1024,1024]{1,0:T(8,128)(2,1)S(1)} collective-permute-done((bf16[1024,1024]{1,0:T(8,128)(2,1)S(1)}, bf16[1024,1024]{1,0:T(8,128)(2,1)S(1)}, u32[]{:S(2)}, u32[]{:S(2)}) %collective-permute-start.2) | collective-permute-done | bytes 2097184 | tf_op jit(solution)/shard_map/ppermute | solution.py:45
  86.5 25.5 %collective-permute-done.3 = bf16[1024,1024]{1,0:T(8,128)(2,1)S(1)} collective-permute-done((bf16[1024,1024]{1,0:T(8,128)(2,1)S(1)}, bf16[1024,1024]{1,0:T(8,128)(2,1)S(1)}, u32[]{:S(2)}, u32[]{:S(2)}) %collective-permute-start.3) | collective-permute-done | bytes 2097184 | tf_op jit(solution)/shard_map/ppermute | solution.py:45
  113.3 25.5 %collective-permute-done.4 = bf16[1024,1024]{1,0:T(8,128)(2,1)S(1)} collective-permute-done((bf16[1024,1024]{1,0:T(8,128)(2,1)S(1)}, bf16[1024,1024]{1,0:T(8,128)(2,1)S(1)}, u32[]{:S(2)}, u32[]{:S(2)}) %collective-permute-start.4) | collective-permute-done | bytes 2097184 | tf_op jit(solution)/shard_map/ppermute | solution.py:45
  140.1 25.6 %collective-permute-done.5 = bf16[1024,1024]{1,0:T(8,128)(2,1)} collective-permute-done((bf16[1024,1024]{1,0:T(8,128)(2,1)S(1)}, bf16[1024,1024]{1,0:T(8,128)(2,1)}, u32[]{:S(2)}, u32[]{:S(2)}) %collective-permute-start.5) | collective-permute-done | bytes 2097184 | tf_op jit(solution)/shard_map/ppermute | solution.py:45
  165.6 6.3 copy.13
  172.7 3.2 fusion.11
  176.1 15.3 %collective-permute-done.6 = bf16[1024,1024]{1,0:T(8,128)(2,1)} collective-permute-done((bf16[1024,1024]{1,0:T(8,128)(2,1)}, bf16[1024,1024]{1,0:T(8,128)(2,1)}, u32[]{:S(2)}, u32[]{:S(2)}) %collective-permute-start.6) | collective-permute-done | bytes 2097184 | tf_op jit(solution)/shard_map/ppermute | solution.py:45
  191.4 3.1 constant_dynamic-update-slice_fusion.15
  194.5 3.2 constant_dynamic-update-slice_fusion.14
  199.2 1.5 constant_dynamic-update-slice_fusion.12
  200.8 1.5 constant_dynamic-update-slice_fusion.11
  206.8 3.1 constant_dynamic-update-slice_fusion.7
  209.9 3.1 constant_dynamic-update-slice_fusion.6
  214.4 1.5 constant_dynamic-update-slice_fusion.4
  216.0 1.5 constant_dynamic-update-slice_fusion.3
  222.0 15.1 %fusion = f32[8192,384]{1,0:T(8,128)} fusion(bf16[384,1024]{1,0:T(8,128)(2,1)S(1)} %copy-done.12, bf16[16384,1024]{1,0:T(8,128)(2,1)} %constant_dynamic-update-slice_fusion, s32[]{:T(128)S(6)} %select_n.41), kind=kOutput, calls=%fused_computation.4 | convolution fusion | flops 6442450944 | bytes 30146564 | tf_op jit(solution)/shard_map/dot_general | solution.py:51
  237.0 8.7 %gather_fusion.1 = f32[40,384,128]{1,2,0:T(8,128)} fusion(f32[384,64,128]{0,2,1:T(8,128)} %bitcast.33, s32[1024]{0:T(1024)S(1)} %get-tuple-element.18), kind=kCustom, calls=%fused_computation.1 | custom fusion | bytes 15728800 | tf_op jit(solution)/shard_map/jit(_take)/gather | solution.py:55
  245.8 7.8 %fusion.14 = (f32[5120]{0:T(1024)S(1)}, f32[384]{0:T(512)S(1)}) fusion(bf16[384,5120]{0,1:T(8,128)(2,1)} %copy.13, f32[40,384,128]{1,2,0:T(8,128)} %gather_fusion.1, f32[384]{0:T(512)S(1)} %add_rsqrt_fusion, pred[5120]{0:T(1024)(128)(4,1)S(1)} %broadcast_bitcast_fusion.2, f32[5120]{0:T(1024)S(1)} %copy-done.13), kind=kLoop, calls=%fused_computation.22 | loop fusion | flops 15723136 | bytes 11845632 | tf_op jit(solution)/shard_map/reduce_sum | solution.py:71
  253.6 5.5 fusion.10
  259.1 6.3 copy.14
  265.4 6.1 gather_fusion
  271.4 8.6 %copy.15 = bf16[384,64,128]{0,2,1:T(8,128)(2,1)} copy(bf16[384,64,128]{2,0,1:T(8,128)(2,1)} %bitcast.31) | data formatting | bytes 12582912 | tf_op jit(solution)/shard_map/jit(_take)/gather | solution.py:39
  280.1 6.9 %fusion.16 = bf16[384,8192]{0,1:T(8,128)(2,1)S(1)} fusion(bf16[384,64,128]{0,2,1:T(8,128)(2,1)} %copy.15, pred[8192]{0:T(1024)(128)(4,1)S(1)} %get-tuple-element.20, pred[8192]{0:T(1024)(128)(4,1)S(1)} %get-tuple-element.21), kind=kLoop, calls=%fused_computation.26 | loop fusion | flops 6291456 | bytes 12599296 | tf_op jit(solution)/shard_map/jit(_where)/select_n | solution.py:40
  287.0 2.6 copy-done.11
  289.6 11.7 %multiply_convert_fusion = bf16[8192,1024]{1,0:T(8,128)(2,1)} fusion(bf16[384,8192]{0,1:T(8,128)(2,1)S(1)} %fusion.16, bf16[384,1024]{1,0:T(8,128)(2,1)S(1)} %copy-done.12), kind=kOutput, calls=%fused_computation.3 | convolution fusion | flops 6459228160 | bytes 23855104 | tf_op jit(solution)/shard_map/dot_general | solution.py:62
  301.4 6.5 %copy.16 = bf16[384,5120]{1,0:T(8,128)(2,1)} copy(bf16[384,5120]{0,1:T(8,128)(2,1)} %get-tuple-element.14) | data formatting | bytes 7864320
  307.9 52.8 %all-reduce = (f32[5120]{0:T(1024)}, f32[1024]{0:T(1024)}) all-reduce(f32[5120]{0:T(1024)S(1)} %broadcast_multiply_fusion, f32[1024]{0:T(1024)S(1)} %broadcast_multiply_fusion.1), channel_id=1, replica_groups=mesh['shard'=8,'rep'=4] {'shard','rep'}, use_global_device_ids=true, to_apply=%region_6.7 | all-reduce | flops 6144 | bytes 49152 | tf_op jit(solution)/shard_map/psum | solution.py:74
  360.7 13.0 %add_convert_fusion = bf16[384,1024]{1,0:T(8,128)(2,1)} fusion(bf16[384,8192]{0,1:T(8,128)(2,1)} %copy-done.11, bf16[16384,1024]{1,0:T(8,128)(2,1)} %constant_dynamic-update-slice_fusion, s32[]{:T(128)S(6)} %select_n.41, f32[1024]{0:T(1024)S(1)} %copy-done.14), kind=kOutput, calls=%fused_computation.28 | convolution fusion | flops 6443237376 | bytes 23859204 | tf_op jit(solution)/shard_map/dot_general | solution.py:50
  373.7 105.0 %reduce-scatter.2.cloned.1.call-done = bf16[1024,1024]{1,0:T(8,128)(2,1)} async-done(((bf16[8192,1024]{1,0:T(8,128)(2,1)}), bf16[1024,1024]{1,0:T(8,128)(2,1)}) %reduce-scatter.2.cloned.1.call-update) | async-done | bytes 2097168 | tf_op jit(solution)/shard_map/reduce_scatter | solution.py:60
  478.8 146.8 %all-reduce.2 = f32[1024,1024]{1,0:T(8,128)} all-reduce(bf16[1024,1024]{1,0:T(8,128)(2,1)} %reduce-scatter.2.cloned.1.call-done), channel_id=1, replica_groups=mesh['shard'=8,'rep'=4] {'rep'}, use_global_device_ids=true, to_apply=%region_4.5 | all-reduce | flops 1048576 | bytes 6291456 | tf_op jit(solution)/shard_map/psum | solution.py:73
  (62 shorter events, 18.4 us)
Async XLA Ops:
  7.2 164.7 %copy-start.15 = (s32[40]{0:T(128)S(1)}, s32[40]{0:T(128)}, u32[]{:S(2)}) copy-start(s32[40]{0:T(128)} %param.11) | copy-start | bytes 484
  7.2 471.6 %reduce-scatter.2.cloned.1.call-start = ((), (), s32[]{:S(2)}) async-start(), calls=%async_computation.1 | async-start | bytes 18874368 | tf_op jit(solution)/shard_map/reduce_scatter | solution.py:60
  7.2 25.7 %collective-permute-start = (bf16[1024,1024]{1,0:T(8,128)(2,1)}, bf16[1024,1024]{1,0:T(8,128)(2,1)S(1)}, u32[]{:S(2)}, u32[]{:S(2)}) collective-permute-start(bf16[1024,1024]{1,0:T(8,128)(2,1)} %param.9), channel_id=1, source_target_pairs={{0,4},{4,8},{8,12},{12,16},{16,20},{20,24},{24,28},{28,0},{1,5},{5... | collective-permute-start | bytes 6291464 | tf_op jit(solution)/shard_map/ppermute | solution.py:45
  32.9 25.5 %collective-permute-start.1 = (bf16[1024,1024]{1,0:T(8,128)(2,1)S(1)}, bf16[1024,1024]{1,0:T(8,128)(2,1)S(1)}, u32[]{:S(2)}, u32[]{:S(2)}) collective-permute-start(bf16[1024,1024]{1,0:T(8,128)(2,1)S(1)} %collective-permute-done), channel_id=1, source_target_pairs={{0,4},{4,8},{8,12},{12,16},{16,20},{20,24},{24,28},{28,0},{1,5},{5... | collective-permute-start | bytes 6291464 | tf_op jit(solution)/shard_map/ppermute | solution.py:45
  58.4 1.3 copy-start.3
  59.7 25.5 %collective-permute-start.2 = (bf16[1024,1024]{1,0:T(8,128)(2,1)S(1)}, bf16[1024,1024]{1,0:T(8,128)(2,1)S(1)}, u32[]{:S(2)}, u32[]{:S(2)}) collective-permute-start(bf16[1024,1024]{1,0:T(8,128)(2,1)S(1)} %collective-permute-done.1), channel_id=1, source_target_pairs={{0,4},{4,8},{8,12},{12,16},{16,20},{20,24},{24,28},{28,0},{1,5},{5... | collective-permute-start | bytes 6291464 | tf_op jit(solution)/shard_map/ppermute | solution.py:45
  85.2 1.3 copy-start.5
  86.5 25.5 %collective-permute-start.3 = (bf16[1024,1024]{1,0:T(8,128)(2,1)S(1)}, bf16[1024,1024]{1,0:T(8,128)(2,1)S(1)}, u32[]{:S(2)}, u32[]{:S(2)}) collective-permute-start(bf16[1024,1024]{1,0:T(8,128)(2,1)S(1)} %collective-permute-done.2), channel_id=1, source_target_pairs={{0,4},{4,8},{8,12},{12,16},{16,20},{20,24},{24,28},{28,0},{1,5},{5... | collective-permute-start | bytes 6291464 | tf_op jit(solution)/shard_map/ppermute | solution.py:45
  111.9 1.4 copy-start.7
  113.3 25.5 %collective-permute-start.4 = (bf16[1024,1024]{1,0:T(8,128)(2,1)S(1)}, bf16[1024,1024]{1,0:T(8,128)(2,1)S(1)}, u32[]{:S(2)}, u32[]{:S(2)}) collective-permute-start(bf16[1024,1024]{1,0:T(8,128)(2,1)S(1)} %collective-permute-done.3), channel_id=1, source_target_pairs={{0,4},{4,8},{8,12},{12,16},{16,20},{20,24},{24,28},{28,0},{1,5},{5... | collective-permute-start | bytes 6291464 | tf_op jit(solution)/shard_map/ppermute | solution.py:45
  138.8 1.3 copy-start.9
  140.1 25.6 %collective-permute-start.5 = (bf16[1024,1024]{1,0:T(8,128)(2,1)S(1)}, bf16[1024,1024]{1,0:T(8,128)(2,1)}, u32[]{:S(2)}, u32[]{:S(2)}) collective-permute-start(bf16[1024,1024]{1,0:T(8,128)(2,1)S(1)} %collective-permute-done.4), channel_id=1, source_target_pairs={{0,4},{4,8},{8,12},{12,16},{16,20},{20,24},{24,28},{28,0},{1,5},{5... | collective-permute-start | bytes 6291464 | tf_op jit(solution)/shard_map/ppermute | solution.py:45
  165.6 25.8 %collective-permute-start.6 = (bf16[1024,1024]{1,0:T(8,128)(2,1)}, bf16[1024,1024]{1,0:T(8,128)(2,1)}, u32[]{:S(2)}, u32[]{:S(2)}) collective-permute-start(bf16[1024,1024]{1,0:T(8,128)(2,1)} %collective-permute-done.5), channel_id=1, source_target_pairs={{0,4},{4,8},{8,12},{12,16},{16,20},{20,24},{24,28},{28,0},{1,5},{5... | collective-permute-start | bytes 6291464 | tf_op jit(solution)/shard_map/ppermute | solution.py:45
  172.6 25.1 %copy-start.10 = (bf16[1024,1024]{1,0:T(8,128)(2,1)S(1)}, bf16[1024,1024]{1,0:T(8,128)(2,1)}, u32[]{:S(2)}) copy-start(bf16[1024,1024]{1,0:T(8,128)(2,1)} %copy-done.9) | copy-start | bytes 6291460
  172.7 26.5 %copy-start.8 = (bf16[1024,1024]{1,0:T(8,128)(2,1)S(1)}, bf16[1024,1024]{1,0:T(8,128)(2,1)}, u32[]{:S(2)}) copy-start(bf16[1024,1024]{1,0:T(8,128)(2,1)} %copy-done.7) | copy-start | bytes 6291460
  176.1 24.7 %copy-start.6 = (bf16[1024,1024]{1,0:T(8,128)(2,1)S(1)}, bf16[1024,1024]{1,0:T(8,128)(2,1)}, u32[]{:S(2)}) copy-start(bf16[1024,1024]{1,0:T(8,128)(2,1)} %copy-done.5) | copy-start | bytes 6291460
  194.5 7.8 %copy-start.4 = (bf16[1024,1024]{1,0:T(8,128)(2,1)S(1)}, bf16[1024,1024]{1,0:T(8,128)(2,1)}, u32[]{:S(2)}) copy-start(bf16[1024,1024]{1,0:T(8,128)(2,1)} %copy-done.3) | copy-start | bytes 6291460
  199.2 6.1 copy-start.2
  216.0 6.0 copy-start.12
  237.0 8.7 %copy-start.13 = (f32[5120]{0:T(1024)S(1)}, f32[5120]{0:T(1024)}, u32[]{:S(2)}) copy-start(f32[5120]{0:T(1024)} %param.7) | copy-start | bytes 61444
  245.8 7.9 %copy-start = (f32[40,384,128]{1,2,0:T(8,128)S(1)}, f32[40,384,128]{1,2,0:T(8,128)}, u32[]{:S(2)}) copy-start(f32[40,384,128]{1,2,0:T(8,128)} %gather_fusion.1) | copy-start | bytes 23592964
  245.8 7.9 %copy-start.1 = (bf16[384,5120]{0,1:T(8,128)(2,1)S(1)}, bf16[384,5120]{0,1:T(8,128)(2,1)}, u32[]{:S(2)}) copy-start(bf16[384,5120]{0,1:T(8,128)(2,1)} %copy.13) | copy-start | bytes 11796484
  287.0 2.6 copy-start.11
  301.2 59.5 %copy-start.14 = (f32[1024]{0:T(1024)S(1)}, f32[1024]{0:T(1024)}, u32[]{:S(2)}) copy-start(f32[1024]{0:T(1024)} %param.8) | copy-start | bytes 12292
Sparse Core Ops, SparseCore 0:
  301.4 177.3 reduce-scatter.1
